TPU v7x, 128 devices: a whole 4x4x4 slice. The times are simulated.
128 devices in a mesh: dp: 2 (over core), emb: 64 (over z, y, x).
Axes of the slice: x: 4, y: 4, z: 4, core: 2. Of those that a mesh axis runs over, the one named last changes fastest.
Arguments:
- tok_ids: int32 [32768], P(('dp', 'emb'))
- resid_in: bfloat16 [32768, 1152], P(('dp', 'emb'))
- cot_out: bfloat16 [32768, 1152], P(('dp', 'emb'))
- tables: bfloat16 [3, 262144, 256], P(None, 'emb')
- w_up: bfloat16 [3, 1152, 6912], replicated
- w_down: bfloat16 [3, 6912, 1152], replicated
- w_gate: bfloat16 [3, 1152, 256], replicated
- w_proj: bfloat16 [3, 256, 1152], replicated
Outputs:
- output 1: bfloat16 [32768, 1152], P(('dp', 'emb'))
- output 2: float32 [3, 262144, 256], P(None, 'emb')
All inputs are finite; a program needn't handle non-finite values.
Results may differ from a plain program's by a relative error of at most 0.012038.
Values are sent between devices in bfloat16 or wider.
A program may use at most 1 GiB of HBM per device.

v0:
```python
import functools
import math

import jax
import jax.numpy as jnp
from jax import lax
from jax.experimental import pallas as pl
from jax.experimental.pallas import tpu as pltpu
from jax.sharding import PartitionSpec as P

NORM_EPS = 1e-6
CAP = 8
BF = jnp.bfloat16
F32 = jnp.float32
MESH_ID = pl.DeviceIdType.MESH
VMEM_LIMIT = 67_043_328
GELU_C = math.sqrt(2.0 / math.pi)


def dot(a, b):
    return jnp.dot(a, b, preferred_element_type=F32)


def dot_nt(a, b):
    return lax.dot_general(a, b, (((1,), (1,)), ((), ())), preferred_element_type=F32)


def dot_tn(a, b):
    return lax.dot_general(a, b, (((0,), (0,)), ((), ())), preferred_element_type=F32)


def iota(shape, axis):
    return lax.broadcasted_iota(jnp.int32, shape, axis)


def gelu_both(x):
    x2 = x * x
    t = jnp.tanh(x * (GELU_C + (GELU_C * 0.044715) * x2))
    hx = 0.5 * x
    s = 0.5 + 0.5 * t
    d = s + hx * (1.0 - t * t) * (GELU_C + (3.0 * GELU_C * 0.044715) * x2)
    return x * s, d


def inv_rms(x):
    return lax.rsqrt(jnp.mean(x * x, axis=-1, keepdims=True) + NORM_EPS)


def peers_barrier(n_emb):
    me, dp = lax.axis_index("emb"), lax.axis_index("dp")
    bar = pltpu.get_barrier_semaphore()

    def tell(k, carry):
        pl.semaphore_signal(bar, inc=1, device_id={"emb": lax.rem(me + k, n_emb)}, device_id_type=MESH_ID)
        return carry

    lax.fori_loop(1, n_emb, tell, 0)
    pl.semaphore_signal(bar, inc=1, device_id={"dp": 1 - dp}, device_id_type=MESH_ID)
    return bar


def send_blocks(n_emb, src, dst, send_sem, recv_sem):
    me = lax.axis_index("emb")

    def one(k, carry):
        to = lax.rem(me + k, n_emb)
        pltpu.make_async_remote_copy(
            src_ref=src.at[to], dst_ref=dst.at[me], send_sem=send_sem, recv_sem=recv_sem,
            device_id={"emb": to}, device_id_type=MESH_ID).start()
        return carry

    lax.fori_loop(1, n_emb, one, 0)


def blocks_desc(n_emb, src, dst, send_sem, recv_sem):
    me = lax.axis_index("emb")
    return pltpu.make_async_remote_copy(
        src_ref=src.at[pl.ds(0, n_emb - 1)], dst_ref=dst.at[pl.ds(0, n_emb - 1)],
        send_sem=send_sem, recv_sem=recv_sem, device_id={"emb": me}, device_id_type=MESH_ID)


def partner_copy(src, dst, send_sem, recv_sem):
    return pltpu.make_async_remote_copy(
        src_ref=src, dst_ref=dst, send_sem=send_sem, recv_sem=recv_sem,
        device_id={"dp": 1 - lax.axis_index("dp")}, device_id_type=MESH_ID)


RING = 6
GROUP = 3


def step_kernel(n_layers, n_emb, ids_ref, resid_hbm, cot_hbm, table_hbm, up_hbm, down_hbm, gate_hbm, proj_hbm,
                out_hbm, rows_hbm, rid_ref,
                wup, wdn, gate, proj, gp, acc, xs, us, cots, hid, gval, gder, fetched,
                table, st, sid, rid, served, fetch_in, grad_out, grad_in,
                upsem, dnsem, ldsem, tsem, isem, psem, fsem, gsem, dsem, wsem):
    me = lax.axis_index("emb")
    n_rows, e = table.shape[1:]
    t, d = acc.shape
    tf = wup.shape[2]
    n_slots = n_emb * CAP
    n_chunks = up_hbm.shape[2] // tf
    n_groups = n_chunks // GROUP
    total = (2 * n_layers - 1) * n_chunks

    def layer_of(g):
        p = g // n_chunks
        return jnp.minimum(p, 2 * n_layers - 1 - p)

    def up_copy(g):
        c, s = lax.rem(g, n_chunks), lax.rem(g, RING)
        return pltpu.make_async_copy(up_hbm.at[layer_of(g), :, pl.ds(pl.multiple_of(c * tf, tf), tf)],
                                     wup.at[s], upsem.at[s])

    def dn_copy(g):
        c, s = lax.rem(g, n_chunks), lax.rem(g, RING)
        return pltpu.make_async_copy(down_hbm.at[layer_of(g), pl.ds(pl.multiple_of(c * tf, tf), tf), :],
                                     wdn.at[s], dnsem.at[s])

    load_x = pltpu.make_async_copy(resid_hbm, xs.at[0], ldsem.at[0])
    load_gate = pltpu.make_async_copy(gate_hbm, gate, ldsem.at[1])
    load_proj = pltpu.make_async_copy(proj_hbm, proj, ldsem.at[2])
    load_cot = pltpu.make_async_copy(cot_hbm, cots, ldsem.at[3])
    load_table = [pltpu.make_async_copy(table_hbm.at[l], table.at[l], tsem.at[l]) for l in range(n_layers)]
    load_x.start()
    load_gate.start()
    for g in range(GROUP):
        up_copy(jnp.int32(g)).start()
        dn_copy(jnp.int32(g)).start()
    for ld in load_table:
        ld.start()
    load_proj.start()
    for g in range(GROUP, RING):
        up_copy(jnp.int32(g)).start()
        dn_copy(jnp.int32(g)).start()
    load_cot.start()
    bar = peers_barrier(n_emb)


    ids = ids_ref[...]
    shift = n_rows.bit_length() - 1
    owner = lax.shift_right_logical(ids, shift)
    local = ids - lax.shift_left(owner, shift) + 1
    own_t = owner == iota((n_emb, t), 0)
    before = (iota((t, t), 0) < iota((t, t), 1)).astype(F32).astype(BF)
    own_f = own_t.astype(F32)
    rank = jnp.sum(own_f * dot(own_f.astype(BF), before), axis=0, keepdims=True).astype(jnp.int32)
    st[...] = (owner * CAP + rank == iota((n_slots, t), 0)).astype(F32).astype(BF)
    rank_t = (rank == iota((128, t), 0)).astype(F32).astype(BF)
    id_hi = jnp.where(own_t, lax.shift_right_logical(local, 6).astype(F32), 0.0).astype(BF)
    id_lo = jnp.where(own_t, jnp.bitwise_and(local, 63).astype(F32), 0.0).astype(BF)
    sid[...] = (64.0 * dot_nt(id_hi, rank_t) + dot_nt(id_lo, rank_t)).astype(jnp.int32).reshape(sid.shape)

    def send_ids():
        pl.semaphore_wait(bar, n_emb)
        send_blocks(n_emb, sid, rid, isem.at[0], isem.at[1])

    ids_to_partner = partner_copy(rid_ref.at[0], rid_ref.at[1], psem.at[0], psem.at[1])

    def serve():
        blocks_desc(n_emb, sid, rid, isem.at[0], isem.at[1]).wait()
        rid[me] = sid[me]
        ids_in = rid[...].reshape(n_emb, 128)
        spread = (lax.shift_right_logical(iota((n_slots, n_emb), 0), 3) == iota((n_slots, n_emb), 1))
        spread = spread.astype(F32).astype(BF)
        hi = lax.shift_right_logical(ids_in, 6).astype(F32).astype(BF)
        lo = jnp.bitwise_and(ids_in, 63).astype(F32).astype(BF)
        pick = jnp.bitwise_and(iota((n_slots, 128), 0), CAP - 1) == iota((n_slots, 128), 1)
        col_hi = jnp.sum(jnp.where(pick, dot(spread, hi), 0.0), axis=1, keepdims=True)
        col_lo = jnp.sum(jnp.where(pick, dot(spread, lo), 0.0), axis=1, keepdims=True)
        col = (64.0 * col_hi + col_lo).astype(jnp.int32) - 1
        chunk = min(1024, n_rows)
        for l in range(n_layers):
            load_table[l].wait()
            sel = None
            for c in range(n_rows // chunk):
                oh = (col == iota((n_slots, chunk), 1) + c * chunk).astype(F32).astype(BF)
                part = dot(oh, table[l, c * chunk:(c + 1) * chunk, :])
                sel = part if sel is None else sel + part
            served[l] = sel.astype(BF).reshape(n_emb, CAP, e)
            send_blocks(n_emb, served.at[l], fetch_in.at[l], fsem.at[0, l], fsem.at[1, l])
        lane = jnp.bitwise_and(iota((n_slots, 128), 0), 127) == iota((n_slots, 128), 1)
        row = (lax.shift_right_logical(iota((8, n_slots), 1), 7) == iota((8, n_slots), 0)).astype(F32).astype(BF)
        flat_hi = dot(row, jnp.where(lane, col_hi, 0.0).astype(BF))
        flat_lo = dot(row, jnp.where(lane, col_lo, 0.0).astype(BF))
        rid_ref[0] = (64.0 * flat_hi + flat_lo).astype(jnp.int32)
        ids_to_partner.start()


    def begin_forward(l):
        x = xs[l].astype(F32)
        us[...] = (x * inv_rms(x)).astype(BF)
        g, der = gelu_both(dot(us[...], gate[l]))
        gval[l] = g
        gder[l] = der
        acc[...] = x

    n_sub = tf // 256

    def fwd_up(l, g, c, k):
        w = wup.at[lax.rem(g, RING)]
        for j in range(n_sub):
            cols = slice(j * 256, (j + 1) * 256)
            h, der = gelu_both(dot(us[...], w[:, cols]))
            hid[k, :, cols] = h.astype(BF)
            gp[lax.rem(l + 1, 2), c, :, cols] = der
        up_copy(g + RING).start()

    def fwd_down(g, k):
        acc[...] += dot(hid[k], wdn[lax.rem(g, RING)])
        dn_copy(g + RING).start()

    def wait_group(g):
        for k in range(GROUP):
            up_copy(g + k).wait()
            dn_copy(g + k).wait()

    def end_forward(l):
        for q in range(n_layers):
            @pl.when(l == q)
            def _():
                blocks_desc(n_emb, served.at[q], fetch_in.at[q], fsem.at[0, q], fsem.at[1, q]).wait()
        fetch_in[l, me] = served[l, me]
        fetched[l] = dot_tn(st[...], fetch_in[l].reshape(n_slots, e)).astype(BF)
        mixed = (gval[l] * fetched[l].astype(F32)).astype(BF)
        xs[l + 1] = (acc[...] + dot(mixed, proj[l])).astype(BF)

    def forward(i, carry):
        l, c0 = i // n_groups, lax.rem(i, n_groups) * GROUP
        g = i * GROUP

        @pl.when(c0 == 0)
        def _():
            begin_forward(l)

        @pl.when(i == 1)
        def _():
            send_ids()

        @pl.when(i == 2)
        def _():
            serve()

        wait_group(g)
        fwd_up(l, g, c0, 0)
        fwd_up(l, g + 1, c0 + 1, 1)
        fwd_down(g, 0)
        fwd_up(l, g + 2, c0 + 2, 2)
        fwd_down(g + 1, 1)
        fwd_down(g + 2, 2)

        @pl.when(c0 == n_chunks - GROUP)
        def _():
            end_forward(l)

        return carry

    load_x.wait()
    load_gate.wait()
    load_proj.wait()
    lax.fori_loop(0, n_layers * n_groups, forward, 0)
    write_out = pltpu.make_async_copy(xs.at[n_layers], out_hbm, wsem.at[0])
    write_out.start()
    load_cot.wait()


    def send_grads(l):
        d_mixed = dot_nt(cots[...], proj[l]).astype(BF).astype(F32)
        rows = gval[l] * d_mixed
        hi = rows.astype(BF)
        rest = rows - hi.astype(F32)
        mid = rest.astype(BF)
        low = (rest - mid.astype(F32)).astype(BF)
        slots = dot(st[...], hi) + dot(st[...], mid) + dot(st[...], low)
        grad_out[l] = slots.reshape(grad_out.shape[1:])
        send_blocks(n_emb, grad_out.at[l], grad_in.at[l], gsem.at[0, l], gsem.at[1, l])
        return d_mixed

    def to_partner(l):
        return partner_copy(grad_in.at[l], rows_hbm.at[1, l], dsem.at[0, l], dsem.at[1, l])

    def to_hbm(l):
        return pltpu.make_async_copy(grad_in.at[l], rows_hbm.at[0, l], wsem.at[1 + l])

    def hand_over(l):
        blocks_desc(n_emb, grad_out.at[l], grad_in.at[l], gsem.at[0, l], gsem.at[1, l]).wait()
        grad_in[l, me] = grad_out[l, me]
        to_partner(l).start()
        to_hbm(l).start()

    def begin_backward(l):
        d_mixed = send_grads(l)
        d_gate = (gder[l] * (d_mixed * fetched[l].astype(F32))).astype(BF)
        us[...] = dot_nt(d_gate, gate[l]).astype(BF)
        acc[...] = jnp.zeros_like(acc)

    def bwd_down(l, g, c, k):
        w = wdn.at[lax.rem(g, RING)]
        for j in range(n_sub):
            cols = slice(j * 256, (j + 1) * 256)
            dh = dot_nt(cots[...], w[cols, :]).astype(BF).astype(F32)
            hid[k, :, cols] = (gp[lax.rem(l + 1, 2), c, :, cols] * dh).astype(BF)

    def bwd_up(g, k):
        acc[...] += dot_nt(hid[k], wup[lax.rem(g, RING)])

    def end_backward(l):
        d_norm = (acc[...].astype(BF).astype(F32) + us[...].astype(F32)).astype(BF).astype(F32)
        x = xs[l].astype(F32)
        r = inv_rms(x)
        dx = r * d_norm - x * (r * r * r * jnp.mean(x * d_norm, axis=-1, keepdims=True))
        cots[...] = (cots[...].astype(F32) + dx).astype(BF)

    def backward(i, carry):
        l, c0 = n_layers - 1 - i // n_groups, lax.rem(i, n_groups) * GROUP
        g = (n_layers * n_groups + i) * GROUP

        @pl.when(c0 == 0)
        def _():
            begin_backward(l)

        wait_group(g)
        bwd_down(l, g, c0, 0)
        bwd_down(l, g + 1, c0 + 1, 1)
        bwd_up(g, 0)

        @pl.when(g + RING < total)
        def _():
            dn_copy(g + RING).start()
            up_copy(g + RING).start()
            dn_copy(g + 1 + RING).start()

        bwd_down(l, g + 2, c0 + 2, 2)
        bwd_up(g + 1, 1)
        bwd_up(g + 2, 2)

        @pl.when(g + RING < total)
        def _():
            up_copy(g + 1 + RING).start()
            dn_copy(g + 2 + RING).start()
            up_copy(g + 2 + RING).start()

        @pl.when(c0 == n_chunks - GROUP)
        def _():
            end_backward(l)
            for q in range(1, n_layers):
                @pl.when(l == q)
                def _():
                    hand_over(q)

        return carry

    lax.fori_loop(0, (n_layers - 1) * n_groups, backward, 0)
    send_grads(0)
    hand_over(0)
    ids_to_partner.wait()
    write_out.wait()
    for l in reversed(range(n_layers)):
        to_hbm(l).wait()
        to_partner(l).wait()


def step(n_emb, tok_ids, resid, cot, tables, w_up, w_down, w_gate, w_proj, tf):
    t, d = resid.shape
    n_layers, n_rows, e = tables.shape
    f = w_up.shape[2]
    n_slots = n_emb * CAP
    vmem, hbm = pl.BlockSpec(memory_space=pltpu.VMEM), pl.BlockSpec(memory_space=pl.ANY)
    dma = pltpu.SemaphoreType.DMA
    return pl.pallas_call(
        functools.partial(step_kernel, n_layers, n_emb),
        out_shape=(jax.ShapeDtypeStruct((t, d), BF),
                   jax.ShapeDtypeStruct((2, n_layers, n_emb, CAP, e), F32),
                   jax.ShapeDtypeStruct((2, 8, 128), jnp.int32)),
        in_specs=[vmem] + [hbm] * 7,
        out_specs=(hbm, hbm, vmem),
        scratch_shapes=[
            pltpu.VMEM((RING, d, tf), BF),
            pltpu.VMEM((RING, tf, d), BF),
            pltpu.VMEM((n_layers, d, e), BF),
            pltpu.VMEM((n_layers, e, d), BF),
            pltpu.VMEM((2, f // tf, t, tf), F32),
            pltpu.VMEM((t, d), F32),
            pltpu.VMEM((n_layers + 1, t, d), BF),
            pltpu.VMEM((t, d), BF),
            pltpu.VMEM((t, d), BF),
            pltpu.VMEM((GROUP, t, tf), BF),
            pltpu.VMEM((n_layers, t, e), F32),
            pltpu.VMEM((n_layers, t, e), F32),
            pltpu.VMEM((n_layers, t, e), BF),
            pltpu.VMEM((n_layers, n_rows, e), BF),
            pltpu.VMEM((n_slots, t), BF),
            pltpu.VMEM((n_emb, 1, 128), jnp.int32),
            pltpu.VMEM((n_emb, 1, 128), jnp.int32),
            pltpu.VMEM((n_layers, n_emb, CAP, e), BF),
            pltpu.VMEM((n_layers, n_emb, CAP, e), BF),
            pltpu.VMEM((n_layers, n_emb, CAP, e), F32),
            pltpu.VMEM((n_layers, n_emb, CAP, e), F32),
            dma((RING,)), dma((RING,)), dma((4,)), dma((n_layers,)), dma((2,)), dma((2,)),
            dma((2, n_layers)), dma((2, n_layers)), dma((2, n_layers)), dma((1 + n_layers,)),
        ],
        compiler_params=pltpu.CompilerParams(collective_id=0, has_side_effects=True, vmem_limit_bytes=VMEM_LIMIT),
        name="step",
    )(tok_ids.reshape(1, t), resid, cot, tables, w_up, w_down, w_gate, w_proj)


def scatter_kernel(n_layers, n_rows, ids_ref, rows_hbm, out_hbm, rows, *scratch):
    acc, (insem, sem) = scratch[:n_layers], scratch[n_layers:]
    e = rows.shape[4]
    n_emb = rows.shape[2]
    load = pltpu.make_async_copy(rows_hbm, rows, insem)
    load.start()

    def clear(i, carry):
        for l in range(n_layers):
            acc[l][pl.ds(pl.multiple_of(i * 64, 64), 64), :] = jnp.zeros((64, e), F32)
        return carry

    lax.fori_loop(0, n_rows // 64, clear, 0)
    load.wait()

    for half in range(2):
        def block(b, carry):
            s = b * CAP
            i, j = lax.shift_right_logical(s, 7), jnp.bitwise_and(s, 127)
            for k in range(0, CAP, 2):
                v, w = ids_ref[half, i, j + k], ids_ref[half, i, j + k + 1]
                v, w = jnp.where(v > 0, v - 1, n_rows), jnp.where(w > 0, w - 1, n_rows + 1)
                same = v == w
                for l in range(n_layers):
                    first, second = rows[half, l, b, k:k + 1, :], rows[half, l, b, k + 1:k + 2, :]
                    at_v, at_w = acc[l][pl.ds(v, 1), :], acc[l][pl.ds(w, 1), :]
                    acc[l][pl.ds(v, 1), :] = at_v + first
                    acc[l][pl.ds(w, 1), :] = at_w + (second + jnp.where(same, first, 0.0))
            return carry

        lax.fori_loop(0, n_emb, block, 0)
    outs = [pltpu.make_async_copy(acc[l].at[pl.ds(0, n_rows)], out_hbm.at[l], sem.at[l]) for l in range(n_layers)]
    for cp in outs:
        cp.start()
    for cp in outs:
        cp.wait()


def scatter(ids, rows, n_rows):
    _, n_layers, n_emb, _, e = rows.shape
    return pl.pallas_call(
        functools.partial(scatter_kernel, n_layers, n_rows),
        out_shape=jax.ShapeDtypeStruct((n_layers, n_rows, e), F32),
        in_specs=[pl.BlockSpec(memory_space=pltpu.SMEM), pl.BlockSpec(memory_space=pl.ANY)],
        out_specs=pl.BlockSpec(memory_space=pl.ANY),
        scratch_shapes=[pltpu.VMEM(rows.shape, F32)] + [pltpu.VMEM((n_rows + 8, e), F32)] * n_layers
        + [pltpu.SemaphoreType.DMA, pltpu.SemaphoreType.DMA((n_layers,))],
        compiler_params=pltpu.CompilerParams(vmem_limit_bytes=VMEM_LIMIT),
        name="scatter",
    )(ids, rows)


def solution(mesh):
    n_emb = mesh.shape["emb"]
    tok_spec = P(("dp", "emb"))
    act_spec = P(("dp", "emb"), None)
    table_spec = P(None, "emb", None)
    full_spec = P(None, None, None)

    def device_body(tok_ids, resid_in, cot_out, tables, w_up, w_down, w_gate, w_proj):
        f = w_up.shape[2]
        tf = 768 if f % (9 * 768) == 0 else 256
        resid_out, rows, ids = step(n_emb, tok_ids, resid_in, cot_out, tables, w_up, w_down, w_gate, w_proj, tf)
        return resid_out, scatter(ids, rows, tables.shape[1])

    return jax.shard_map(device_body, mesh=mesh,
                         in_specs=(tok_spec, act_spec, act_spec, table_spec, full_spec, full_spec, full_spec, full_spec),
                         out_specs=(act_spec, table_spec), check_vma=False)
```

profile of v0, /device:TPU:1, one launch (start us, length us, event | category | flops | bytes accessed | tf_op | source)
XLA Modules:
  0.0 117.7 jit_solution(9259880358715868233)
XLA Ops:
  0.6 101.1 %step.1 = (bf16[256,1152]{1,0:T(8,128)(2,1)}, f32[2,3,64,8,256]{4,3,2,1,0:T(8,128)}, s32[2,8,128]{2,1,0:T(8,128)}) custom-call(s32[1,256]{1,0:T(1,128)} %bitcast.1, bf16[256,1152]{1,0:T(8,128)(2,1)} %resid_hbm.1, bf16[256,1152]{1,0:T(8,128)(2,1)} %cot_hbm.1, bf16[3,4096,256]{2,1,0:T(8,128)(2,1)} %table_hbm.1, bf16[3,1152,6912]{2,1,0:T(8,128)(2,1)} %up_hbm.1, ...), custom_call_target="tpu_custom_call" | custom-call | tf_op jit(solution)/shard_map/step/pallas_call | solution.py:370
  101.8 14.1 %scatter.1 = f32[3,4096,256]{2,1,0:T(8,128)} custom-call(s32[2,8,128]{2,1,0:T(8,128)} %get-tuple-element.6.ids_ref, f32[2,3,64,8,256]{4,3,2,1,0:T(8,128)} %get-tuple-element.7.rows_hbm), custom_call_target="tpu_custom_call" | custom-call | tf_op jit(solution)/shard_map/scatter/pallas_call | solution.py:447
  115.8 1.9 %copy.11 = bf16[256,1152]{1,0:T(8,128)(2,1)} copy(bf16[256,1152]{1,0:T(8,128)(2,1)} %get-tuple-element.10) | data formatting | bytes 1179648
where the time goes:
time: 118 us
  Pallas kernels  115 us (97%)
  local copies, waits for them, and re-layouts  1.92 us (2%)
    pallas_call x1, Pallas kernels, step(): pl.pallas_call(functools.partial(step_kernel, n_layers, n_emb), out_shape...  101 us
    pallas_call x1, Pallas kernels, scatter(): pl.pallas_call(functools.partial(scatter_kernel, n_layers, n_rows), out_s...  14.1 us

commit v1 on v0

--- a/solution.py
+++ b/solution.py
@@ -107,33 +107,32 @@
         p = g // n_chunks
         return jnp.minimum(p, 2 * n_layers - 1 - p)
 
+    def chunk_of(g):
+        turn = jnp.where(g // n_chunks == n_layers, n_chunks - RING, 0)
+        return lax.rem(g + turn, n_chunks)
+
     def up_copy(g):
-        c, s = lax.rem(g, n_chunks), lax.rem(g, RING)
+        c, s = chunk_of(g), lax.rem(g, RING)
         return pltpu.make_async_copy(up_hbm.at[layer_of(g), :, pl.ds(pl.multiple_of(c * tf, tf), tf)],
                                      wup.at[s], upsem.at[s])
 
     def dn_copy(g):
-        c, s = lax.rem(g, n_chunks), lax.rem(g, RING)
+        c, s = chunk_of(g), lax.rem(g, RING)
         return pltpu.make_async_copy(down_hbm.at[layer_of(g), pl.ds(pl.multiple_of(c * tf, tf), tf), :],
                                      wdn.at[s], dnsem.at[s])
 
     load_x = pltpu.make_async_copy(resid_hbm, xs.at[0], ldsem.at[0])
-    load_gate = pltpu.make_async_copy(gate_hbm, gate, ldsem.at[1])
+    load_cot = pltpu.make_async_copy(cot_hbm, cots, ldsem.at[1])
     load_proj = pltpu.make_async_copy(proj_hbm, proj, ldsem.at[2])
-    load_cot = pltpu.make_async_copy(cot_hbm, cots, ldsem.at[3])
+    load_gate = [pltpu.make_async_copy(gate_hbm.at[l], gate.at[l], ldsem.at[3 + l]) for l in range(n_layers)]
     load_table = [pltpu.make_async_copy(table_hbm.at[l], table.at[l], tsem.at[l]) for l in range(n_layers)]
     load_x.start()
-    load_gate.start()
-    for g in range(GROUP):
+    load_gate[0].start()
+    for g in range(RING):
         up_copy(jnp.int32(g)).start()
         dn_copy(jnp.int32(g)).start()
-    for ld in load_table:
+    for ld in load_table + [load_proj] + load_gate[1:] + [load_cot]:
         ld.start()
-    load_proj.start()
-    for g in range(GROUP, RING):
-        up_copy(jnp.int32(g)).start()
-        dn_copy(jnp.int32(g)).start()
-    load_cot.start()
     bar = peers_barrier(n_emb)
 
 
@@ -183,7 +182,9 @@
         row = (lax.shift_right_logical(iota((8, n_slots), 1), 7) == iota((8, n_slots), 0)).astype(F32).astype(BF)
         flat_hi = dot(row, jnp.where(lane, col_hi, 0.0).astype(BF))
         flat_lo = dot(row, jnp.where(lane, col_lo, 0.0).astype(BF))
-        rid_ref[0] = (64.0 * flat_hi + flat_lo).astype(jnp.int32)
+        flat = (64.0 * flat_hi + flat_lo).astype(jnp.int32) - 1
+        spare = n_rows + jnp.bitwise_and(iota(flat.shape, 1), 1)
+        rid_ref[0] = jnp.where(flat < 0, spare, flat)
         ids_to_partner.start()
 
 
@@ -197,18 +198,20 @@
 
     n_sub = tf // 256
 
-    def fwd_up(l, g, c, k):
+    def fwd_up(l, g, c, k, more):
         w = wup.at[lax.rem(g, RING)]
         for j in range(n_sub):
             cols = slice(j * 256, (j + 1) * 256)
             h, der = gelu_both(dot(us[...], w[:, cols]))
             hid[k, :, cols] = h.astype(BF)
             gp[lax.rem(l + 1, 2), c, :, cols] = der
-        up_copy(g + RING).start()
-
-    def fwd_down(g, k):
+        if more:
+            up_copy(g + RING).start()
+
+    def fwd_down(g, k, more):
         acc[...] += dot(hid[k], wdn[lax.rem(g, RING)])
-        dn_copy(g + RING).start()
+        if more:
+            dn_copy(g + RING).start()
 
     def wait_group(g):
         for k in range(GROUP):
@@ -220,34 +223,36 @@
             @pl.when(l == q)
             def _():
                 blocks_desc(n_emb, served.at[q], fetch_in.at[q], fsem.at[0, q], fsem.at[1, q]).wait()
+        @pl.when(l == 0)
+        def _():
+            for ld in [load_proj] + load_gate[1:]:
+                ld.wait()
+
         fetch_in[l, me] = served[l, me]
         fetched[l] = dot_tn(st[...], fetch_in[l].reshape(n_slots, e)).astype(BF)
         mixed = (gval[l] * fetched[l].astype(F32)).astype(BF)
         xs[l + 1] = (acc[...] + dot(mixed, proj[l])).astype(BF)
 
-    def forward(i, carry):
+    def forward(more, i, carry):
         l, c0 = i // n_groups, lax.rem(i, n_groups) * GROUP
         g = i * GROUP
 
-        @pl.when(c0 == 0)
-        def _():
-            begin_forward(l)
-
-        @pl.when(i == 1)
-        def _():
-            send_ids()
-
-        @pl.when(i == 2)
-        def _():
-            serve()
+        if more:
+            @pl.when(c0 == 0)
+            def _():
+                begin_forward(l)
+
+            @pl.when(i == 2)
+            def _():
+                serve()
 
         wait_group(g)
-        fwd_up(l, g, c0, 0)
-        fwd_up(l, g + 1, c0 + 1, 1)
-        fwd_down(g, 0)
-        fwd_up(l, g + 2, c0 + 2, 2)
-        fwd_down(g + 1, 1)
-        fwd_down(g + 2, 2)
+        fwd_up(l, g, c0, 0, more)
+        fwd_up(l, g + 1, c0 + 1, 1, more)
+        fwd_down(g, 0, more)
+        fwd_up(l, g + 2, c0 + 2, 2, more)
+        fwd_down(g + 1, 1, more)
+        fwd_down(g + 2, 2, more)
 
         @pl.when(c0 == n_chunks - GROUP)
         def _():
@@ -256,9 +261,18 @@
         return carry
 
     load_x.wait()
-    load_gate.wait()
-    load_proj.wait()
-    lax.fori_loop(0, n_layers * n_groups, forward, 0)
+    load_gate[0].wait()
+    begin_forward(0)
+    for k in range(GROUP):
+        g = jnp.int32(k)
+        up_copy(g).wait()
+        fwd_up(0, g, k, k, True)
+        dn_copy(g).wait()
+        fwd_down(g, k, True)
+    send_ids()
+    kept = n_layers * n_groups - RING // GROUP
+    lax.fori_loop(1, kept, functools.partial(forward, True), 0)
+    lax.fori_loop(kept, n_layers * n_groups, functools.partial(forward, False), 0)
     write_out = pltpu.make_async_copy(xs.at[n_layers], out_hbm, wsem.at[0])
     write_out.start()
     load_cot.wait()
@@ -312,14 +326,18 @@
         cots[...] = (cots[...].astype(F32) + dx).astype(BF)
 
     def backward(i, carry):
-        l, c0 = n_layers - 1 - i // n_groups, lax.rem(i, n_groups) * GROUP
+        l, place = n_layers - 1 - i // n_groups, lax.rem(i, n_groups)
         g = (n_layers * n_groups + i) * GROUP
-
-        @pl.when(c0 == 0)
+        c0 = chunk_of(g)
+
+        @pl.when(place == 0)
         def _():
             begin_backward(l)
 
-        wait_group(g)
+        @pl.when(i >= RING // GROUP)
+        def _():
+            wait_group(g)
+
         bwd_down(l, g, c0, 0)
         bwd_down(l, g + 1, c0 + 1, 1)
         bwd_up(g, 0)
@@ -340,7 +358,7 @@
             dn_copy(g + 2 + RING).start()
             up_copy(g + 2 + RING).start()
 
-        @pl.when(c0 == n_chunks - GROUP)
+        @pl.when(place == n_groups - 1)
         def _():
             end_backward(l)
             for q in range(1, n_layers):
@@ -396,7 +414,7 @@
             pltpu.VMEM((n_layers, n_emb, CAP, e), BF),
             pltpu.VMEM((n_layers, n_emb, CAP, e), F32),
             pltpu.VMEM((n_layers, n_emb, CAP, e), F32),
-            dma((RING,)), dma((RING,)), dma((4,)), dma((n_layers,)), dma((2,)), dma((2,)),
+            dma((RING,)), dma((RING,)), dma((3 + n_layers,)), dma((n_layers,)), dma((2,)), dma((2,)),
             dma((2, n_layers)), dma((2, n_layers)), dma((2, n_layers)), dma((1 + n_layers,)),
         ],
         compiler_params=pltpu.CompilerParams(collective_id=0, has_side_effects=True, vmem_limit_bytes=VMEM_LIMIT),
@@ -404,12 +422,15 @@
     )(tok_ids.reshape(1, t), resid, cot, tables, w_up, w_down, w_gate, w_proj)
 
 
-def scatter_kernel(n_layers, n_rows, ids_ref, rows_hbm, out_hbm, rows, *scratch):
-    acc, (insem, sem) = scratch[:n_layers], scratch[n_layers:]
+def scatter_kernel(n_layers, n_rows, ids_ref, rows_hbm, x_hbm, out_hbm, x_out, rows, x, *scratch):
+    acc, (insem, xsem, sem) = scratch[:n_layers], scratch[n_layers:]
     e = rows.shape[4]
     n_emb = rows.shape[2]
-    load = pltpu.make_async_copy(rows_hbm, rows, insem)
-    load.start()
+    loads = [pltpu.make_async_copy(rows_hbm.at[h], rows.at[h], insem.at[h]) for h in range(2)]
+    x_in = pltpu.make_async_copy(x_hbm, x, xsem.at[0])
+    x_back = pltpu.make_async_copy(x, x_out, xsem.at[1])
+    for ld in loads + [x_in]:
+        ld.start()
 
     def clear(i, carry):
         for l in range(n_layers):
@@ -417,43 +438,48 @@
         return carry
 
     lax.fori_loop(0, n_rows // 64, clear, 0)
-    load.wait()
+    per_row = min(128 // CAP, n_emb)
 
     for half in range(2):
-        def block(b, carry):
-            s = b * CAP
-            i, j = lax.shift_right_logical(s, 7), jnp.bitwise_and(s, 127)
-            for k in range(0, CAP, 2):
-                v, w = ids_ref[half, i, j + k], ids_ref[half, i, j + k + 1]
-                v, w = jnp.where(v > 0, v - 1, n_rows), jnp.where(w > 0, w - 1, n_rows + 1)
-                same = v == w
-                for l in range(n_layers):
-                    first, second = rows[half, l, b, k:k + 1, :], rows[half, l, b, k + 1:k + 2, :]
-                    at_v, at_w = acc[l][pl.ds(v, 1), :], acc[l][pl.ds(w, 1), :]
-                    acc[l][pl.ds(v, 1), :] = at_v + first
-                    acc[l][pl.ds(w, 1), :] = at_w + (second + jnp.where(same, first, 0.0))
-            return carry
-
-        lax.fori_loop(0, n_emb, block, 0)
+        loads[half].wait()
+        if half == 1:
+            x_in.wait()
+            x_back.start()
+        for i in range(n_emb // per_row):
+            def block(p, carry):
+                b = i * per_row + p
+                for k in range(0, CAP, 2):
+                    v, w = ids_ref[half, i, p * CAP + k], ids_ref[half, i, p * CAP + k + 1]
+                    same = v == w
+                    for l in range(n_layers):
+                        first, second = rows[half, l, b, k:k + 1, :], rows[half, l, b, k + 1:k + 2, :]
+                        at_v, at_w = acc[l][pl.ds(v, 1), :], acc[l][pl.ds(w, 1), :]
+                        acc[l][pl.ds(v, 1), :] = at_v + first
+                        acc[l][pl.ds(w, 1), :] = at_w + (second + jnp.where(same, first, 0.0))
+                return carry
+
+            lax.fori_loop(0, per_row, block, 0)
     outs = [pltpu.make_async_copy(acc[l].at[pl.ds(0, n_rows)], out_hbm.at[l], sem.at[l]) for l in range(n_layers)]
     for cp in outs:
         cp.start()
-    for cp in outs:
+    for cp in outs + [x_back]:
         cp.wait()
 
 
-def scatter(ids, rows, n_rows):
+def scatter(ids, rows, x, n_rows):
     _, n_layers, n_emb, _, e = rows.shape
+    hbm = pl.BlockSpec(memory_space=pl.ANY)
     return pl.pallas_call(
         functools.partial(scatter_kernel, n_layers, n_rows),
-        out_shape=jax.ShapeDtypeStruct((n_layers, n_rows, e), F32),
-        in_specs=[pl.BlockSpec(memory_space=pltpu.SMEM), pl.BlockSpec(memory_space=pl.ANY)],
-        out_specs=pl.BlockSpec(memory_space=pl.ANY),
-        scratch_shapes=[pltpu.VMEM(rows.shape, F32)] + [pltpu.VMEM((n_rows + 8, e), F32)] * n_layers
-        + [pltpu.SemaphoreType.DMA, pltpu.SemaphoreType.DMA((n_layers,))],
+        out_shape=(jax.ShapeDtypeStruct((n_layers, n_rows, e), F32), jax.ShapeDtypeStruct(x.shape, x.dtype)),
+        in_specs=[pl.BlockSpec(memory_space=pltpu.SMEM), hbm, hbm],
+        out_specs=(hbm, hbm),
+        scratch_shapes=[pltpu.VMEM(rows.shape, F32), pltpu.VMEM(x.shape, x.dtype)]
+        + [pltpu.VMEM((n_rows + 8, e), F32)] * n_layers
+        + [pltpu.SemaphoreType.DMA((2,)), pltpu.SemaphoreType.DMA((2,)), pltpu.SemaphoreType.DMA((n_layers,))],
         compiler_params=pltpu.CompilerParams(vmem_limit_bytes=VMEM_LIMIT),
         name="scatter",
-    )(ids, rows)
+    )(ids, rows, x)
 
 
 def solution(mesh):
@@ -467,7 +493,8 @@
         f = w_up.shape[2]
         tf = 768 if f % (9 * 768) == 0 else 256
         resid_out, rows, ids = step(n_emb, tok_ids, resid_in, cot_out, tables, w_up, w_down, w_gate, w_proj, tf)
-        return resid_out, scatter(ids, rows, tables.shape[1])
+        d_tables, resid_out = scatter(ids, rows, resid_out, tables.shape[1])
+        return resid_out, d_tables
 
     return jax.shard_map(device_body, mesh=mesh,
                          in_specs=(tok_spec, act_spec, act_spec, table_spec, full_spec, full_spec, full_spec, full_spec),

time: 118 us -> 111 us (0.941)
  Pallas kernels: 115 us -> 110 us
  local copies, waits for them, and re-layouts: 1.92 us -> 0 us
    pallas_call x1, Pallas kernels: 101 us -> 97.5 us  [step(): pl.pallas_call(functools.partial(step_kernel, n_layers, n_emb), out_shape...]
    unnamed x1 -> x0, local copies, waits for them, and re-layouts: 1.92 us -> none
    pallas_call x1, Pallas kernels: 14.1 us -> 12.6 us  [scatter(): pl.pallas_call(functools.partial(scatter_kernel, n_layers, n_rows), out_s...]
where the time goes in v1:
time: 111 us
  Pallas kernels  110 us (99%)
    pallas_call x1, Pallas kernels, step(): pl.pallas_call(functools.partial(step_kernel, n_layers, n_emb), out_shape...  97.5 us
    pallas_call x1, Pallas kernels, scatter(): pl.pallas_call(functools.partial(scatter_kernel, n_layers, n_rows), out_s...  12.6 us

profile of v1, /device:TPU:1, one launch (start us, length us, event | category | flops | bytes accessed | tf_op | source)
XLA Modules:
  0.0 111.0 jit_solution(12161741106540191802)
XLA Ops:
  0.6 97.5 %step.1 = (bf16[256,1152]{1,0:T(8,128)(2,1)}, f32[2,3,64,8,256]{4,3,2,1,0:T(8,128)}, s32[2,8,128]{2,1,0:T(8,128)}) custom-call(s32[1,256]{1,0:T(1,128)} %bitcast.1, bf16[256,1152]{1,0:T(8,128)(2,1)} %resid_hbm.1, bf16[256,1152]{1,0:T(8,128)(2,1)} %cot_hbm.1, bf16[3,4096,256]{2,1,0:T(8,128)(2,1)} %table_hbm.1, bf16[3,1152,6912]{2,1,0:T(8,128)(2,1)} %up_hbm.1, ...), custom_call_target="tpu_custom_call" | custom-call | tf_op jit(solution)/shard_map/step/pallas_call | solution.py:388
  98.2 12.6 %scatter.1 = (f32[3,4096,256]{2,1,0:T(8,128)}, bf16[256,1152]{1,0:T(8,128)(2,1)}) custom-call(s32[2,8,128]{2,1,0:T(8,128)} %get-tuple-element.7.ids_ref, f32[2,3,64,8,256]{4,3,2,1,0:T(8,128)} %get-tuple-element.8.rows_hbm, bf16[256,1152]{1,0:T(8,128)(2,1)} %get-tuple-element.9.x_hbm), custom_call_target="tpu_custom_call" | custom-call | tf_op jit(solution)/shard_map/scatter/pallas_call | solution.py:472

commit v2 on v1

--- a/solution.py
+++ b/solution.py
@@ -93,9 +93,10 @@
                 out_hbm, rows_hbm, rid_ref,
                 wup, wdn, gate, proj, gp, acc, xs, us, cots, hid, gval, gder, fetched,
                 table, st, sid, rid, served, fetch_in, grad_out, grad_in,
-                upsem, dnsem, ldsem, tsem, isem, psem, fsem, gsem, dsem, wsem):
+                ringsem, ldsem, tsem, isem, psem, fsem, gsem, dsem, wsem, msem):
     me = lax.axis_index("emb")
     n_rows, e = table.shape[1:]
+    t_chunk = min(1024, n_rows)
     t, d = acc.shape
     tf = wup.shape[2]
     n_slots = n_emb * CAP
@@ -104,33 +105,45 @@
     total = (2 * n_layers - 1) * n_chunks
 
     def layer_of(g):
+        if isinstance(g, int):
+            return 0
         p = g // n_chunks
         return jnp.minimum(p, 2 * n_layers - 1 - p)
 
     def chunk_of(g):
+        if isinstance(g, int):
+            return g
         turn = jnp.where(g // n_chunks == n_layers, n_chunks - RING, 0)
         return lax.rem(g + turn, n_chunks)
 
+    def slot_of(g):
+        return g % RING if isinstance(g, int) else lax.rem(g, RING)
+
+    def ring_sem(g):
+        if isinstance(g, int) and g < GROUP:
+            return ringsem.at[2 + min(g, 1)]
+        return ringsem.at[lax.rem(g // GROUP, 2)]
+
     def up_copy(g):
-        c, s = chunk_of(g), lax.rem(g, RING)
-        return pltpu.make_async_copy(up_hbm.at[layer_of(g), :, pl.ds(pl.multiple_of(c * tf, tf), tf)],
-                                     wup.at[s], upsem.at[s])
+        c, s = chunk_of(g), slot_of(g)
+        return pltpu.make_async_copy(up_hbm.at[layer_of(g), :, pl.ds(c * tf if isinstance(c, int) else pl.multiple_of(c * tf, tf), tf)],
+                                     wup.at[s], ring_sem(g))
 
     def dn_copy(g):
-        c, s = chunk_of(g), lax.rem(g, RING)
-        return pltpu.make_async_copy(down_hbm.at[layer_of(g), pl.ds(pl.multiple_of(c * tf, tf), tf), :],
-                                     wdn.at[s], dnsem.at[s])
+        c, s = chunk_of(g), slot_of(g)
+        return pltpu.make_async_copy(down_hbm.at[layer_of(g), pl.ds(c * tf if isinstance(c, int) else pl.multiple_of(c * tf, tf), tf), :],
+                                     wdn.at[s], ring_sem(g))
 
     load_x = pltpu.make_async_copy(resid_hbm, xs.at[0], ldsem.at[0])
     load_cot = pltpu.make_async_copy(cot_hbm, cots, ldsem.at[1])
     load_proj = pltpu.make_async_copy(proj_hbm, proj, ldsem.at[2])
     load_gate = [pltpu.make_async_copy(gate_hbm.at[l], gate.at[l], ldsem.at[3 + l]) for l in range(n_layers)]
-    load_table = [pltpu.make_async_copy(table_hbm.at[l], table.at[l], tsem.at[l]) for l in range(n_layers)]
+    load_table = [pltpu.make_async_copy(table_hbm.at[l], table.at[l % 2], tsem.at[l]) for l in range(min(n_layers, 2))]
     load_x.start()
     load_gate[0].start()
     for g in range(RING):
-        up_copy(jnp.int32(g)).start()
-        dn_copy(jnp.int32(g)).start()
+        up_copy(g).start()
+        dn_copy(g).start()
     for ld in load_table + [load_proj] + load_gate[1:] + [load_cot]:
         ld.start()
     bar = peers_barrier(n_emb)
@@ -168,13 +181,16 @@
         col_hi = jnp.sum(jnp.where(pick, dot(spread, hi), 0.0), axis=1, keepdims=True)
         col_lo = jnp.sum(jnp.where(pick, dot(spread, lo), 0.0), axis=1, keepdims=True)
         col = (64.0 * col_hi + col_lo).astype(jnp.int32) - 1
-        chunk = min(1024, n_rows)
+        chunk = t_chunk
         for l in range(n_layers):
-            load_table[l].wait()
+            pltpu.make_async_copy(table_hbm.at[l], table.at[l % 2], tsem.at[l]).wait()
             sel = None
             for c in range(n_rows // chunk):
                 oh = (col == iota((n_slots, chunk), 1) + c * chunk).astype(F32).astype(BF)
-                part = dot(oh, table[l, c * chunk:(c + 1) * chunk, :])
+                part = dot(oh, table[l % 2, c * chunk:(c + 1) * chunk, :])
+                if l + 2 < n_layers:
+                    piece = pl.ds(c * chunk, chunk)
+                    pltpu.make_async_copy(table_hbm.at[l + 2, piece], table.at[l % 2, piece], tsem.at[l + 2]).start()
                 sel = part if sel is None else sel + part
             served[l] = sel.astype(BF).reshape(n_emb, CAP, e)
             send_blocks(n_emb, served.at[l], fetch_in.at[l], fsem.at[0, l], fsem.at[1, l])
@@ -187,6 +203,15 @@
         rid_ref[0] = jnp.where(flat < 0, spare, flat)
         ids_to_partner.start()
 
+    def send_rows(l, rows):
+        hi = rows.astype(BF)
+        rest = rows - hi.astype(F32)
+        mid = rest.astype(BF)
+        low = (rest - mid.astype(F32)).astype(BF)
+        slots = dot(st[...], hi) + dot(st[...], mid) + dot(st[...], low)
+        grad_out[l] = slots.reshape(grad_out.shape[1:])
+        send_blocks(n_emb, grad_out.at[l], grad_in.at[l], gsem.at[0, l], gsem.at[1, l])
+
 
     def begin_forward(l):
         x = xs[l].astype(F32)
@@ -213,10 +238,11 @@
         if more:
             dn_copy(g + RING).start()
 
+    def wait_chunks(n, sem):
+        pltpu.make_async_copy(wup.at[pl.ds(0, 2 * n)], wup.at[pl.ds(0, 2 * n)], sem).wait()
+
     def wait_group(g):
-        for k in range(GROUP):
-            up_copy(g + k).wait()
-            dn_copy(g + k).wait()
+        wait_chunks(GROUP, ring_sem(g))
 
     def end_forward(l):
         for q in range(n_layers):
@@ -231,7 +257,7 @@
         fetch_in[l, me] = served[l, me]
         fetched[l] = dot_tn(st[...], fetch_in[l].reshape(n_slots, e)).astype(BF)
         mixed = (gval[l] * fetched[l].astype(F32)).astype(BF)
-        xs[l + 1] = (acc[...] + dot(mixed, proj[l])).astype(BF)
+        xs[lax.rem(l + 1, n_layers)] = (acc[...] + dot(mixed, proj[l])).astype(BF)
 
     def forward(more, i, carry):
         l, c0 = i // n_groups, lax.rem(i, n_groups) * GROUP
@@ -245,6 +271,10 @@
             @pl.when(i == 2)
             def _():
                 serve()
+
+            @pl.when(i == n_groups + 2)
+            def _():
+                send_rows(0, gval[0])
 
         wait_group(g)
         fwd_up(l, g, c0, 0, more)
@@ -263,47 +293,59 @@
     load_x.wait()
     load_gate[0].wait()
     begin_forward(0)
-    for k in range(GROUP):
-        g = jnp.int32(k)
-        up_copy(g).wait()
-        fwd_up(0, g, k, k, True)
-        dn_copy(g).wait()
-        fwd_down(g, k, True)
+    wait_chunks(1, ringsem.at[2])
+    fwd_up(0, jnp.int32(0), 0, 0, True)
+    fwd_down(jnp.int32(0), 0, True)
+    wait_chunks(GROUP - 1, ringsem.at[3])
+    for k in range(1, GROUP):
+        fwd_up(0, jnp.int32(k), k, k, True)
+    for k in range(1, GROUP):
+        fwd_down(jnp.int32(k), k, True)
     send_ids()
     kept = n_layers * n_groups - RING // GROUP
     lax.fori_loop(1, kept, functools.partial(forward, True), 0)
     lax.fori_loop(kept, n_layers * n_groups, functools.partial(forward, False), 0)
-    write_out = pltpu.make_async_copy(xs.at[n_layers], out_hbm, wsem.at[0])
+    write_out = pltpu.make_async_copy(xs.at[0], out_hbm, wsem.at[0])
     write_out.start()
     load_cot.wait()
 
 
+    def mixed_grad(l):
+        return dot_nt(cots[...], proj[l]).astype(BF)
+
     def send_grads(l):
-        d_mixed = dot_nt(cots[...], proj[l]).astype(BF).astype(F32)
-        rows = gval[l] * d_mixed
-        hi = rows.astype(BF)
-        rest = rows - hi.astype(F32)
-        mid = rest.astype(BF)
-        low = (rest - mid.astype(F32)).astype(BF)
-        slots = dot(st[...], hi) + dot(st[...], mid) + dot(st[...], low)
-        grad_out[l] = slots.reshape(grad_out.shape[1:])
-        send_blocks(n_emb, grad_out.at[l], grad_in.at[l], gsem.at[0, l], gsem.at[1, l])
+        d_mixed = mixed_grad(l).astype(F32)
+        send_rows(l, gval[l] * d_mixed)
         return d_mixed
+
+    mixed_out, mixed_in = served.at[0], fetch_in.at[0]
 
     def to_partner(l):
         return partner_copy(grad_in.at[l], rows_hbm.at[1, l], dsem.at[0, l], dsem.at[1, l])
 
     def to_hbm(l):
         return pltpu.make_async_copy(grad_in.at[l], rows_hbm.at[0, l], wsem.at[1 + l])
+
+    def mixed_desc():
+        return blocks_desc(n_emb, mixed_out, mixed_in, msem.at[0], msem.at[1])
 
     def hand_over(l):
         blocks_desc(n_emb, grad_out.at[l], grad_in.at[l], gsem.at[0, l], gsem.at[1, l]).wait()
         grad_in[l, me] = grad_out[l, me]
+        if l == 0:
+            mixed_desc().wait()
+            mixed_in[me] = mixed_out[me]
+            grad_in[0] = grad_in[0] * mixed_in[...].astype(F32)
         to_partner(l).start()
         to_hbm(l).start()
 
     def begin_backward(l):
         d_mixed = send_grads(l)
+        for q in range(2, n_layers):
+            @pl.when(l == q - 1)
+            def _():
+                hand_over(q)
+
         d_gate = (gder[l] * (d_mixed * fetched[l].astype(F32))).astype(BF)
         us[...] = dot_nt(d_gate, gate[l]).astype(BF)
         acc[...] = jnp.zeros_like(acc)
@@ -361,15 +403,13 @@
         @pl.when(place == n_groups - 1)
         def _():
             end_backward(l)
-            for q in range(1, n_layers):
-                @pl.when(l == q)
-                def _():
-                    hand_over(q)
 
         return carry
 
     lax.fori_loop(0, (n_layers - 1) * n_groups, backward, 0)
-    send_grads(0)
+    mixed_out[...] = dot(st[...], mixed_grad(0)).astype(BF).reshape(mixed_out.shape)
+    send_blocks(n_emb, mixed_out, mixed_in, msem.at[0], msem.at[1])
+    hand_over(1)
     hand_over(0)
     ids_to_partner.wait()
     write_out.wait()
@@ -399,14 +439,14 @@
             pltpu.VMEM((n_layers, e, d), BF),
             pltpu.VMEM((2, f // tf, t, tf), F32),
             pltpu.VMEM((t, d), F32),
-            pltpu.VMEM((n_layers + 1, t, d), BF),
+            pltpu.VMEM((n_layers, t, d), BF),
             pltpu.VMEM((t, d), BF),
             pltpu.VMEM((t, d), BF),
             pltpu.VMEM((GROUP, t, tf), BF),
             pltpu.VMEM((n_layers, t, e), F32),
             pltpu.VMEM((n_layers, t, e), F32),
             pltpu.VMEM((n_layers, t, e), BF),
-            pltpu.VMEM((n_layers, n_rows, e), BF),
+            pltpu.VMEM((2, n_rows, e), BF),
             pltpu.VMEM((n_slots, t), BF),
             pltpu.VMEM((n_emb, 1, 128), jnp.int32),
             pltpu.VMEM((n_emb, 1, 128), jnp.int32),
@@ -414,8 +454,8 @@
             pltpu.VMEM((n_layers, n_emb, CAP, e), BF),
             pltpu.VMEM((n_layers, n_emb, CAP, e), F32),
             pltpu.VMEM((n_layers, n_emb, CAP, e), F32),
-            dma((RING,)), dma((RING,)), dma((3 + n_layers,)), dma((n_layers,)), dma((2,)), dma((2,)),
-            dma((2, n_layers)), dma((2, n_layers)), dma((2, n_layers)), dma((1 + n_layers,)),
+            dma((4,)), dma((3 + n_layers,)), dma((n_layers,)), dma((2,)), dma((2,)),
+            dma((2, n_layers)), dma((2, n_layers)), dma((2, n_layers)), dma((1 + n_layers,)), dma((2,)),
         ],
         compiler_params=pltpu.CompilerParams(collective_id=0, has_side_effects=True, vmem_limit_bytes=VMEM_LIMIT),
         name="step",

time: 111 us -> 114 us (1.027)
  Pallas kernels: 110 us -> 113 us
    pallas_call x1, Pallas kernels: 97.5 us -> 101 us  [step(): pl.pallas_call(functools.partial(step_kernel, n_layers, n_emb), out_shape...]
where the time goes in v2:
time: 114 us
  Pallas kernels  113 us (99%)
    pallas_call x1, Pallas kernels, step(): pl.pallas_call(functools.partial(step_kernel, n_layers, n_emb), out_shape...  101 us
    pallas_call x1, Pallas kernels, scatter(): pl.pallas_call(functools.partial(scatter_kernel, n_layers, n_rows), out_s...  12.6 us

profile of v2, /device:TPU:1, one launch (start us, length us, event | category | flops | bytes accessed | tf_op | source)
XLA Modules:
  0.0 114.1 jit_solution(15217515316073744813)
XLA Ops:
  0.6 100.7 %step.1 = (bf16[256,1152]{1,0:T(8,128)(2,1)}, f32[2,3,64,8,256]{4,3,2,1,0:T(8,128)}, s32[2,8,128]{2,1,0:T(8,128)}) custom-call(s32[1,256]{1,0:T(1,128)} %bitcast.1, bf16[256,1152]{1,0:T(8,128)(2,1)} %resid_hbm.1, bf16[256,1152]{1,0:T(8,128)(2,1)} %cot_hbm.1, bf16[3,4096,256]{2,1,0:T(8,128)(2,1)} %table_hbm.1, bf16[3,1152,6912]{2,1,0:T(8,128)(2,1)} %up_hbm.1, ...), custom_call_target="tpu_custom_call" | custom-call | tf_op jit(solution)/shard_map/step/pallas_call | solution.py:428
  101.3 12.6 %scatter.1 = (f32[3,4096,256]{2,1,0:T(8,128)}, bf16[256,1152]{1,0:T(8,128)(2,1)}) custom-call(s32[2,8,128]{2,1,0:T(8,128)} %get-tuple-element.7.ids_ref, f32[2,3,64,8,256]{4,3,2,1,0:T(8,128)} %get-tuple-element.8.rows_hbm, bf16[256,1152]{1,0:T(8,128)(2,1)} %get-tuple-element.9.x_hbm), custom_call_target="tpu_custom_call" | custom-call | tf_op jit(solution)/shard_map/scatter/pallas_call | solution.py:512

commit v3 on v2

--- a/solution.py
+++ b/solution.py
@@ -119,20 +119,15 @@
     def slot_of(g):
         return g % RING if isinstance(g, int) else lax.rem(g, RING)
 
-    def ring_sem(g):
-        if isinstance(g, int) and g < GROUP:
-            return ringsem.at[2 + min(g, 1)]
-        return ringsem.at[lax.rem(g // GROUP, 2)]
-
     def up_copy(g):
         c, s = chunk_of(g), slot_of(g)
         return pltpu.make_async_copy(up_hbm.at[layer_of(g), :, pl.ds(c * tf if isinstance(c, int) else pl.multiple_of(c * tf, tf), tf)],
-                                     wup.at[s], ring_sem(g))
+                                     wup.at[s], ringsem.at[0, s])
 
     def dn_copy(g):
         c, s = chunk_of(g), slot_of(g)
         return pltpu.make_async_copy(down_hbm.at[layer_of(g), pl.ds(c * tf if isinstance(c, int) else pl.multiple_of(c * tf, tf), tf), :],
-                                     wdn.at[s], ring_sem(g))
+                                     wdn.at[s], ringsem.at[1, s])
 
     load_x = pltpu.make_async_copy(resid_hbm, xs.at[0], ldsem.at[0])
     load_cot = pltpu.make_async_copy(cot_hbm, cots, ldsem.at[1])
@@ -238,11 +233,10 @@
         if more:
             dn_copy(g + RING).start()
 
-    def wait_chunks(n, sem):
-        pltpu.make_async_copy(wup.at[pl.ds(0, 2 * n)], wup.at[pl.ds(0, 2 * n)], sem).wait()
-
-    def wait_group(g):
-        wait_chunks(GROUP, ring_sem(g))
+    def wait_group(g, first=0, n=GROUP):
+        for k in range(first, first + n):
+            up_copy(g + k).wait()
+            dn_copy(g + k).wait()
 
     def end_forward(l):
         for q in range(n_layers):
@@ -271,10 +265,6 @@
             @pl.when(i == 2)
             def _():
                 serve()
-
-            @pl.when(i == n_groups + 2)
-            def _():
-                send_rows(0, gval[0])
 
         wait_group(g)
         fwd_up(l, g, c0, 0, more)
@@ -293,10 +283,10 @@
     load_x.wait()
     load_gate[0].wait()
     begin_forward(0)
-    wait_chunks(1, ringsem.at[2])
+    wait_group(0, 0, 1)
     fwd_up(0, jnp.int32(0), 0, 0, True)
     fwd_down(jnp.int32(0), 0, True)
-    wait_chunks(GROUP - 1, ringsem.at[3])
+    wait_group(0, 1, GROUP - 1)
     for k in range(1, GROUP):
         fwd_up(0, jnp.int32(k), k, k, True)
     for k in range(1, GROUP):
@@ -308,6 +298,7 @@
     write_out = pltpu.make_async_copy(xs.at[0], out_hbm, wsem.at[0])
     write_out.start()
     load_cot.wait()
+    send_rows(0, gval[0])
 
 
     def mixed_grad(l):
@@ -454,7 +445,7 @@
             pltpu.VMEM((n_layers, n_emb, CAP, e), BF),
             pltpu.VMEM((n_layers, n_emb, CAP, e), F32),
             pltpu.VMEM((n_layers, n_emb, CAP, e), F32),
-            dma((4,)), dma((3 + n_layers,)), dma((n_layers,)), dma((2,)), dma((2,)),
+            dma((2, RING)), dma((3 + n_layers,)), dma((n_layers,)), dma((2,)), dma((2,)),
             dma((2, n_layers)), dma((2, n_layers)), dma((2, n_layers)), dma((1 + n_layers,)), dma((2,)),
         ],
         compiler_params=pltpu.CompilerParams(collective_id=0, has_side_effects=True, vmem_limit_bytes=VMEM_LIMIT),
@@ -488,14 +479,23 @@
         for i in range(n_emb // per_row):
             def block(p, carry):
                 b = i * per_row + p
-                for k in range(0, CAP, 2):
-                    v, w = ids_ref[half, i, p * CAP + k], ids_ref[half, i, p * CAP + k + 1]
-                    same = v == w
-                    for l in range(n_layers):
-                        first, second = rows[half, l, b, k:k + 1, :], rows[half, l, b, k + 1:k + 2, :]
-                        at_v, at_w = acc[l][pl.ds(v, 1), :], acc[l][pl.ds(w, 1), :]
-                        acc[l][pl.ds(v, 1), :] = at_v + first
-                        acc[l][pl.ds(w, 1), :] = at_w + (second + jnp.where(same, first, 0.0))
+
+                def pairs(k0, k1):
+                    for k in range(k0, k1, 2):
+                        v, w = ids_ref[half, i, p * CAP + k], ids_ref[half, i, p * CAP + k + 1]
+                        same = v == w
+                        for l in range(n_layers):
+                            first, second = rows[half, l, b, k:k + 1, :], rows[half, l, b, k + 1:k + 2, :]
+                            at_v, at_w = acc[l][pl.ds(v, 1), :], acc[l][pl.ds(w, 1), :]
+                            acc[l][pl.ds(v, 1), :] = at_v + first
+                            acc[l][pl.ds(w, 1), :] = at_w + (second + jnp.where(same, first, 0.0))
+
+                pairs(0, CAP // 2)
+
+                @pl.when(ids_ref[half, i, p * CAP + CAP // 2] < n_rows)
+                def _():
+                    pairs(CAP // 2, CAP)
+
                 return carry
 
             lax.fori_loop(0, per_row, block, 0)

time: 114 us -> 111 us (0.974)
  Pallas kernels: 113 us -> 110 us
    pallas_call x1, Pallas kernels: 101 us -> 99.2 us  [step(): pl.pallas_call(functools.partial(step_kernel, n_layers, n_emb), out_shape...]
    pallas_call x1, Pallas kernels: 12.6 us -> 11.2 us  [scatter(): pl.pallas_call(functools.partial(scatter_kernel, n_layers, n_rows), out_s...]
where the time goes in v3:
time: 111 us
  Pallas kernels  110 us (99%)
    pallas_call x1, Pallas kernels, step(): pl.pallas_call(functools.partial(step_kernel, n_layers, n_emb), out_shape...  99.2 us
    pallas_call x1, Pallas kernels, scatter(): pl.pallas_call(functools.partial(scatter_kernel, n_layers, n_rows), out_s...  11.2 us

profile of v3, /device:TPU:1, one launch (start us, length us, event | category | flops | bytes accessed | tf_op | source)
XLA Modules:
  0.0 111.2 jit_solution(14667658603495841238)
XLA Ops:
  0.6 99.2 %step.1 = (bf16[256,1152]{1,0:T(8,128)(2,1)}, f32[2,3,64,8,256]{4,3,2,1,0:T(8,128)}, s32[2,8,128]{2,1,0:T(8,128)}) custom-call(s32[1,256]{1,0:T(1,128)} %bitcast.1, bf16[256,1152]{1,0:T(8,128)(2,1)} %resid_hbm.1, bf16[256,1152]{1,0:T(8,128)(2,1)} %cot_hbm.1, bf16[3,4096,256]{2,1,0:T(8,128)(2,1)} %table_hbm.1, bf16[3,1152,6912]{2,1,0:T(8,128)(2,1)} %up_hbm.1, ...), custom_call_target="tpu_custom_call" | custom-call | tf_op jit(solution)/shard_map/step/pallas_call | solution.py:419
  99.9 11.2 %scatter.1 = (f32[3,4096,256]{2,1,0:T(8,128)}, bf16[256,1152]{1,0:T(8,128)(2,1)}) custom-call(s32[2,8,128]{2,1,0:T(8,128)} %get-tuple-element.7.ids_ref, f32[2,3,64,8,256]{4,3,2,1,0:T(8,128)} %get-tuple-element.8.rows_hbm, bf16[256,1152]{1,0:T(8,128)(2,1)} %get-tuple-element.9.x_hbm), custom_call_target="tpu_custom_call" | custom-call | tf_op jit(solution)/shard_map/scatter/pallas_call | solution.py:512

commit v4 on v3

--- a/solution.py
+++ b/solution.py
@@ -133,7 +133,7 @@
     load_cot = pltpu.make_async_copy(cot_hbm, cots, ldsem.at[1])
     load_proj = pltpu.make_async_copy(proj_hbm, proj, ldsem.at[2])
     load_gate = [pltpu.make_async_copy(gate_hbm.at[l], gate.at[l], ldsem.at[3 + l]) for l in range(n_layers)]
-    load_table = [pltpu.make_async_copy(table_hbm.at[l], table.at[l % 2], tsem.at[l]) for l in range(min(n_layers, 2))]
+    load_table = [pltpu.make_async_copy(table_hbm.at[l], table.at[l], tsem.at[l]) for l in range(n_layers)]
     load_x.start()
     load_gate[0].start()
     for g in range(RING):
@@ -176,17 +176,14 @@
         col_hi = jnp.sum(jnp.where(pick, dot(spread, hi), 0.0), axis=1, keepdims=True)
         col_lo = jnp.sum(jnp.where(pick, dot(spread, lo), 0.0), axis=1, keepdims=True)
         col = (64.0 * col_hi + col_lo).astype(jnp.int32) - 1
-        chunk = t_chunk
         for l in range(n_layers):
-            pltpu.make_async_copy(table_hbm.at[l], table.at[l % 2], tsem.at[l]).wait()
-            sel = None
-            for c in range(n_rows // chunk):
-                oh = (col == iota((n_slots, chunk), 1) + c * chunk).astype(F32).astype(BF)
-                part = dot(oh, table[l % 2, c * chunk:(c + 1) * chunk, :])
-                if l + 2 < n_layers:
-                    piece = pl.ds(c * chunk, chunk)
-                    pltpu.make_async_copy(table_hbm.at[l + 2, piece], table.at[l % 2, piece], tsem.at[l + 2]).start()
-                sel = part if sel is None else sel + part
+            load_table[l].wait()
+
+            def piece(c, sel):
+                oh = (col == iota((n_slots, t_chunk), 1) + c * t_chunk).astype(F32).astype(BF)
+                return sel + dot(oh, table[l, pl.ds(pl.multiple_of(c * t_chunk, t_chunk), t_chunk), :])
+
+            sel = lax.fori_loop(0, n_rows // t_chunk, piece, jnp.zeros((n_slots, e), F32))
             served[l] = sel.astype(BF).reshape(n_emb, CAP, e)
             send_blocks(n_emb, served.at[l], fetch_in.at[l], fsem.at[0, l], fsem.at[1, l])
         lane = jnp.bitwise_and(iota((n_slots, 128), 0), 127) == iota((n_slots, 128), 1)
@@ -437,7 +434,7 @@
             pltpu.VMEM((n_layers, t, e), F32),
             pltpu.VMEM((n_layers, t, e), F32),
             pltpu.VMEM((n_layers, t, e), BF),
-            pltpu.VMEM((2, n_rows, e), BF),
+            pltpu.VMEM((n_layers, n_rows, e), BF),
             pltpu.VMEM((n_slots, t), BF),
             pltpu.VMEM((n_emb, 1, 128), jnp.int32),
             pltpu.VMEM((n_emb, 1, 128), jnp.int32),

time: 111 us -> 111 us (level)
  no operation moved by 1% of the time
where the time goes in v4:
time: 111 us
  Pallas kernels  110 us (99%)
    pallas_call x1, Pallas kernels, step(): pl.pallas_call(functools.partial(step_kernel, n_layers, n_emb), out_shape...  99 us
    pallas_call x1, Pallas kernels, scatter(): pl.pallas_call(functools.partial(scatter_kernel, n_layers, n_rows), out_s...  11.2 us

profile of v4, /device:TPU:1, one launch (start us, length us, event | category | flops | bytes accessed | tf_op | source)
XLA Modules:
  0.0 111.1 jit_solution(16841457972285845789)
XLA Ops:
  0.6 99.0 %step.1 = (bf16[256,1152]{1,0:T(8,128)(2,1)}, f32[2,3,64,8,256]{4,3,2,1,0:T(8,128)}, s32[2,8,128]{2,1,0:T(8,128)}) custom-call(s32[1,256]{1,0:T(1,128)} %bitcast.1, bf16[256,1152]{1,0:T(8,128)(2,1)} %resid_hbm.1, bf16[256,1152]{1,0:T(8,128)(2,1)} %cot_hbm.1, bf16[3,4096,256]{2,1,0:T(8,128)(2,1)} %table_hbm.1, bf16[3,1152,6912]{2,1,0:T(8,128)(2,1)} %up_hbm.1, ...), custom_call_target="tpu_custom_call" | custom-call | tf_op jit(solution)/shard_map/step/pallas_call | solution.py:416
  99.7 11.2 %scatter.1 = (f32[3,4096,256]{2,1,0:T(8,128)}, bf16[256,1152]{1,0:T(8,128)(2,1)}) custom-call(s32[2,8,128]{2,1,0:T(8,128)} %get-tuple-element.7.ids_ref, f32[2,3,64,8,256]{4,3,2,1,0:T(8,128)} %get-tuple-element.8.rows_hbm, bf16[256,1152]{1,0:T(8,128)(2,1)} %get-tuple-element.9.x_hbm), custom_call_target="tpu_custom_call" | custom-call | tf_op jit(solution)/shard_map/scatter/pallas_call | solution.py:509
